TPU v7x, 32 devices: a whole 2x2x4 slice. The times are simulated.
32 devices in a mesh: clients: 8 (over z, x), shard: 4 (over y, core).
Axes of the slice: x: 2, y: 2, z: 4, core: 2. Of those that a mesh axis runs over, the one named last changes fastest.
Arguments:
- quantized: int32 [8, 2097152], P('clients', 'shard'), may hold values from 0 to 2097151
- pair_masks: int32 [8, 2097152], P('clients', 'shard'), may hold values from 0 to 2097142, as said below
- alive_flags: int32 [8], P('clients'), may hold values from 0 to 1, as said below
- row_seeds: int32 [64], replicated, may hold values from 0 to 1073741823
Outputs:
- aggregate: int32 [2097152], P('shard')
- commitments: int32 [8, 64], P('clients')
- mismatch: int32 [64], replicated
Inputs may be any that keep to these rules, and one draw needn't show every extreme that they name: For every position, the pair_masks of all 8 participants sum to a multiple of 2097143. `alive_flags`: at least one participant has flag 1 and at least one has flag 0.
All inputs are finite; a program needn't handle non-finite values.
Results may differ from a plain program's by a relative error of at most 0.000001.
Values may be sent and summed in bfloat16 or wider, within the bound.
A program may use at most 64 MiB of HBM per device.

v0:
```python
import math

import jax
import jax.numpy as jnp
from jax import lax
from jax.sharding import PartitionSpec as P

modulus = 2097143


def table_entries(row_seeds, columns):
    mixed = columns[None, :] * 747796405 + row_seeds[:, None]
    mixed = mixed & 2147483647
    mixed = mixed ^ mixed >> 15
    mixed = mixed * 277803737 & 2147483647
    mixed = mixed ^ mixed >> 13
    mixed = mixed * 1103515245 & 2147483647
    mixed = mixed ^ mixed >> 16
    return mixed & 1023


def project_mod(row_seeds, vectors, offset, block_width):
    vec_count = vectors.shape[0]
    length = vectors.shape[1]
    row_count = row_seeds.shape[0]
    sub_width = math.gcd(block_width, 512)
    block_count = length // block_width

    def advance(running, block_index):
        start_col = block_index * block_width
        columns = offset + start_col + jnp.arange(block_width, dtype=jnp.int32)
        table = table_entries(row_seeds, columns)
        right_part = lax.dynamic_slice_in_dim(vectors, start_col, block_width, 1)
        products = right_part[:, None, :] * table[None, :, :] % modulus
        products = products.reshape(vec_count, row_count, block_width // sub_width, sub_width)
        partial_value = jnp.sum(products, axis=3, dtype=jnp.int32) % modulus
        partial_value = jnp.sum(partial_value, axis=2, dtype=jnp.int32) % modulus
        return ((running + partial_value) % modulus, None)

    running = jnp.zeros((vec_count, row_count), jnp.int32)
    running, unused = lax.scan(advance, running, jnp.arange(block_count, dtype=jnp.int32))
    return running


def block_size(length):
    return length // 16


def body(quantized, pair_masks, alive_flags, row_seeds):
    alive_now = alive_flags[0]
    length = quantized.shape[1]
    masked = (quantized[0] + pair_masks[0]) % modulus * alive_now
    share_length = length // lax.axis_size("clients")
    client_index = lax.axis_index("clients")
    summed = lax.psum(masked, "clients")
    aggregate = summed % modulus
    share_piece = lax.dynamic_slice_in_dim(aggregate, client_index * share_length, share_length, 0)
    offset = lax.axis_index("shard") * length
    own_part = project_mod(row_seeds, quantized, offset, block_size(length))[0]
    own_total = lax.psum(own_part, "shard") % modulus
    commitments = own_total[None, :]
    piece_start = offset + client_index * share_length
    projected_part = project_mod(
        row_seeds, share_piece[None, :], piece_start, block_size(share_length)
    )[0]
    weighted = own_total * alive_now
    projected = lax.psum(projected_part, ("clients", "shard")) % modulus
    expected = lax.psum(weighted, "clients") % modulus
    mismatch = (projected - expected) % modulus
    return (aggregate, commitments, mismatch)


def solution(mesh):
    placed = (P("clients", "shard"), P("clients", "shard"), P("clients"), P())
    return jax.shard_map(
        body,
        mesh=mesh,
        in_specs=placed,
        out_specs=(P("shard"), P("clients", None), P()),
        check_vma=False,
    )
```

profile of v0, /device:TPU:0, one launch (start us, length us, event | category | flops | bytes accessed | tf_op | source)
XLA Modules:
  0.0 342.2 jit_solution(15196851076049243759)
XLA Ops:
  7.9 10.4 %add_remainder_fusion = s32[1,524288]{1,0:T(1,128)S(1)} fusion(s32[1,524288]{1,0:T(1,128)} %param.8, s32[1,524288]{1,0:T(1,128)} %param.9), kind=kLoop, calls=%fused_computation.43 | loop fusion | flops 1048576 | bytes 6291456 | tf_op jit(solution)/shard_map/jit(remainder)/rem | solution.py:52
  18.3 1.7 fusion.20
  20.6 206.8 %while.26 = (s32[]{:T(128)}, s32[1,64]{1,0:T(1,128)S(1)}, s32[16]{0:T(128)S(1)}, s32[1,524288]{1,0:T(1,128)}, s32[]{:T(128)}, /*index=5*/s32[64]{0:T(128)S(1)}, s32[]{:T(128)}, s32[1]{0:T(128)}, s32[]{:T(128)}, s32[]{:T(128)}) while((s32[]{:T(128)}, s32[1,64]{1,0:T(1,128)S(1)}, s32[16]{0:T(128)S(1)}, s32[1,524288]{1,0:T(1,128)}, ...), condition=%wide.region_4.5_spmd.clone, body=%wide.region_1.4_spmd.clone.sunk | while | flops 44196680 | bytes 951749 | solution.py:41
  21.9 1.2 dynamic-slice_reduce_fusion.4
  23.1 10.3 %fusion.27 = s32[64,64]{1,0:T(8,128)S(1)} fusion(s32[64]{0:T(128)S(1)} %get-tuple-element.328, s32[64,512]{1,0:T(8,128)S(1)} %add_multiply_fusion.4, s32[64,512]{1,0:T(8,128)S(1)} %mul.283), kind=kLoop, calls=%fused_computation.11.clone.1 | loop fusion | flops 44036096 | bytes 278784 | tf_op jit(solution)/shard_map/while/body/eval_jaxpr/reduce_sum | solution.py:36
  34.8 1.2 dynamic-slice_reduce_fusion.4
  36.0 10.3 %fusion.27 = s32[64,64]{1,0:T(8,128)S(1)} fusion(s32[64]{0:T(128)S(1)} %get-tuple-element.328, s32[64,512]{1,0:T(8,128)S(1)} %add_multiply_fusion.4, s32[64,512]{1,0:T(8,128)S(1)} %mul.283), kind=kLoop, calls=%fused_computation.11.clone.1 | loop fusion | flops 44036096 | bytes 278784 | tf_op jit(solution)/shard_map/while/body/eval_jaxpr/reduce_sum | solution.py:36
  46.5 0.6 dynamic_slice.40
  47.8 1.2 dynamic-slice_reduce_fusion.4
  48.9 10.3 %fusion.27 = s32[64,64]{1,0:T(8,128)S(1)} fusion(s32[64]{0:T(128)S(1)} %get-tuple-element.328, s32[64,512]{1,0:T(8,128)S(1)} %add_multiply_fusion.4, s32[64,512]{1,0:T(8,128)S(1)} %mul.283), kind=kLoop, calls=%fused_computation.11.clone.1 | loop fusion | flops 44036096 | bytes 278784 | tf_op jit(solution)/shard_map/while/body/eval_jaxpr/reduce_sum | solution.py:36
  60.7 1.2 dynamic-slice_reduce_fusion.4
  61.9 10.3 %fusion.27 = s32[64,64]{1,0:T(8,128)S(1)} fusion(s32[64]{0:T(128)S(1)} %get-tuple-element.328, s32[64,512]{1,0:T(8,128)S(1)} %add_multiply_fusion.4, s32[64,512]{1,0:T(8,128)S(1)} %mul.283), kind=kLoop, calls=%fused_computation.11.clone.1 | loop fusion | flops 44036096 | bytes 278784 | tf_op jit(solution)/shard_map/while/body/eval_jaxpr/reduce_sum | solution.py:36
  73.6 1.2 dynamic-slice_reduce_fusion.4
  74.8 10.3 %fusion.27 = s32[64,64]{1,0:T(8,128)S(1)} fusion(s32[64]{0:T(128)S(1)} %get-tuple-element.328, s32[64,512]{1,0:T(8,128)S(1)} %add_multiply_fusion.4, s32[64,512]{1,0:T(8,128)S(1)} %mul.283), kind=kLoop, calls=%fused_computation.11.clone.1 | loop fusion | flops 44036096 | bytes 278784 | tf_op jit(solution)/shard_map/while/body/eval_jaxpr/reduce_sum | solution.py:36
  85.3 0.6 dynamic_slice.40
  86.5 1.2 dynamic-slice_reduce_fusion.4
  87.7 10.3 %fusion.27 = s32[64,64]{1,0:T(8,128)S(1)} fusion(s32[64]{0:T(128)S(1)} %get-tuple-element.328, s32[64,512]{1,0:T(8,128)S(1)} %add_multiply_fusion.4, s32[64,512]{1,0:T(8,128)S(1)} %mul.283), kind=kLoop, calls=%fused_computation.11.clone.1 | loop fusion | flops 44036096 | bytes 278784 | tf_op jit(solution)/shard_map/while/body/eval_jaxpr/reduce_sum | solution.py:36
  98.2 0.6 dynamic_slice.40
  99.5 1.2 dynamic-slice_reduce_fusion.4
  100.7 10.3 %fusion.27 = s32[64,64]{1,0:T(8,128)S(1)} fusion(s32[64]{0:T(128)S(1)} %get-tuple-element.328, s32[64,512]{1,0:T(8,128)S(1)} %add_multiply_fusion.4, s32[64,512]{1,0:T(8,128)S(1)} %mul.283), kind=kLoop, calls=%fused_computation.11.clone.1 | loop fusion | flops 44036096 | bytes 278784 | tf_op jit(solution)/shard_map/while/body/eval_jaxpr/reduce_sum | solution.py:36
  111.1 0.6 dynamic_slice.40
  112.4 1.2 dynamic-slice_reduce_fusion.4
  113.6 10.3 %fusion.27 = s32[64,64]{1,0:T(8,128)S(1)} fusion(s32[64]{0:T(128)S(1)} %get-tuple-element.328, s32[64,512]{1,0:T(8,128)S(1)} %add_multiply_fusion.4, s32[64,512]{1,0:T(8,128)S(1)} %mul.283), kind=kLoop, calls=%fused_computation.11.clone.1 | loop fusion | flops 44036096 | bytes 278784 | tf_op jit(solution)/shard_map/while/body/eval_jaxpr/reduce_sum | solution.py:36
  124.0 0.6 dynamic_slice.40
  125.3 1.2 dynamic-slice_reduce_fusion.4
  126.5 10.3 %fusion.27 = s32[64,64]{1,0:T(8,128)S(1)} fusion(s32[64]{0:T(128)S(1)} %get-tuple-element.328, s32[64,512]{1,0:T(8,128)S(1)} %add_multiply_fusion.4, s32[64,512]{1,0:T(8,128)S(1)} %mul.283), kind=kLoop, calls=%fused_computation.11.clone.1 | loop fusion | flops 44036096 | bytes 278784 | tf_op jit(solution)/shard_map/while/body/eval_jaxpr/reduce_sum | solution.py:36
  137.0 0.6 dynamic_slice.40
  138.2 1.2 dynamic-slice_reduce_fusion.4
  139.4 10.3 %fusion.27 = s32[64,64]{1,0:T(8,128)S(1)} fusion(s32[64]{0:T(128)S(1)} %get-tuple-element.328, s32[64,512]{1,0:T(8,128)S(1)} %add_multiply_fusion.4, s32[64,512]{1,0:T(8,128)S(1)} %mul.283), kind=kLoop, calls=%fused_computation.11.clone.1 | loop fusion | flops 44036096 | bytes 278784 | tf_op jit(solution)/shard_map/while/body/eval_jaxpr/reduce_sum | solution.py:36
  149.9 0.6 dynamic_slice.40
  151.2 1.2 dynamic-slice_reduce_fusion.4
  152.3 10.3 %fusion.27 = s32[64,64]{1,0:T(8,128)S(1)} fusion(s32[64]{0:T(128)S(1)} %get-tuple-element.328, s32[64,512]{1,0:T(8,128)S(1)} %add_multiply_fusion.4, s32[64,512]{1,0:T(8,128)S(1)} %mul.283), kind=kLoop, calls=%fused_computation.11.clone.1 | loop fusion | flops 44036096 | bytes 278784 | tf_op jit(solution)/shard_map/while/body/eval_jaxpr/reduce_sum | solution.py:36
  164.1 1.2 dynamic-slice_reduce_fusion.4
  165.3 10.3 %fusion.27 = s32[64,64]{1,0:T(8,128)S(1)} fusion(s32[64]{0:T(128)S(1)} %get-tuple-element.328, s32[64,512]{1,0:T(8,128)S(1)} %add_multiply_fusion.4, s32[64,512]{1,0:T(8,128)S(1)} %mul.283), kind=kLoop, calls=%fused_computation.11.clone.1 | loop fusion | flops 44036096 | bytes 278784 | tf_op jit(solution)/shard_map/while/body/eval_jaxpr/reduce_sum | solution.py:36
  177.0 1.2 dynamic-slice_reduce_fusion.4
  178.2 10.3 %fusion.27 = s32[64,64]{1,0:T(8,128)S(1)} fusion(s32[64]{0:T(128)S(1)} %get-tuple-element.328, s32[64,512]{1,0:T(8,128)S(1)} %add_multiply_fusion.4, s32[64,512]{1,0:T(8,128)S(1)} %mul.283), kind=kLoop, calls=%fused_computation.11.clone.1 | loop fusion | flops 44036096 | bytes 278784 | tf_op jit(solution)/shard_map/while/body/eval_jaxpr/reduce_sum | solution.py:36
  189.9 1.2 dynamic-slice_reduce_fusion.4
  191.1 10.3 %fusion.27 = s32[64,64]{1,0:T(8,128)S(1)} fusion(s32[64]{0:T(128)S(1)} %get-tuple-element.328, s32[64,512]{1,0:T(8,128)S(1)} %add_multiply_fusion.4, s32[64,512]{1,0:T(8,128)S(1)} %mul.283), kind=kLoop, calls=%fused_computation.11.clone.1 | loop fusion | flops 44036096 | bytes 278784 | tf_op jit(solution)/shard_map/while/body/eval_jaxpr/reduce_sum | solution.py:36
  202.9 1.2 dynamic-slice_reduce_fusion.4
  204.0 10.3 %fusion.27 = s32[64,64]{1,0:T(8,128)S(1)} fusion(s32[64]{0:T(128)S(1)} %get-tuple-element.328, s32[64,512]{1,0:T(8,128)S(1)} %add_multiply_fusion.4, s32[64,512]{1,0:T(8,128)S(1)} %mul.283), kind=kLoop, calls=%fused_computation.11.clone.1 | loop fusion | flops 44036096 | bytes 278784 | tf_op jit(solution)/shard_map/while/body/eval_jaxpr/reduce_sum | solution.py:36
  215.8 1.2 dynamic-slice_reduce_fusion.4
  217.0 10.3 %fusion.27 = s32[64,64]{1,0:T(8,128)S(1)} fusion(s32[64]{0:T(128)S(1)} %get-tuple-element.328, s32[64,512]{1,0:T(8,128)S(1)} %add_multiply_fusion.4, s32[64,512]{1,0:T(8,128)S(1)} %mul.283), kind=kLoop, calls=%fused_computation.11.clone.1 | loop fusion | flops 44036096 | bytes 278784 | tf_op jit(solution)/shard_map/while/body/eval_jaxpr/reduce_sum | solution.py:36
  227.4 6.4 %psum.29 = s32[64]{0:T(128)S(1)} all-reduce(s32[64]{0:T(128)S(1)} %bitcast.30), channel_id=1, replica_groups=mesh['clients'=8,'shard'=4] {'shard'}, use_global_device_ids=true, to_apply=%region_5.6 | all-reduce | flops 64 | bytes 512 | tf_op jit(solution)/shard_map/psum | solution.py:60
  234.4 11.6 %psum.31 = s32[64]{0:T(128)S(1)} all-reduce(s32[64]{0:T(128)S(1)} %get-tuple-element.227), channel_id=1, replica_groups=mesh['clients'=8,'shard'=4] {'clients'}, use_global_device_ids=true, to_apply=%region_11.12 | all-reduce | flops 64 | bytes 512 | tf_op jit(solution)/shard_map/psum | solution.py:68
  246.0 2.5 add_select_fusion.4
  248.5 47.8 %while.27 = (s32[]{:T(128)}, s32[1,64]{1,0:T(1,128)S(1)}, s32[16]{0:T(128)S(1)}, s32[1,65536]{1,0:T(1,128)S(1)}, s32[]{:T(128)}, /*index=5*/s32[64]{0:T(128)S(1)}, s32[]{:T(128)}, s32[1]{0:T(128)}, s32[]{:T(128)}, s32[]{:T(128)}) while((s32[]{:T(128)}, s32[1,64]{1,0:T(1,128)S(1)}, s32[16]{0:T(128)S(1)}, s32[1,65536]{1,0:T(1,128)S(1)}, ...), condition=%wide.region_9.10_spmd.clone, body=%wide.region_6.9_spmd.clone.sunk | while | flops 5525320 | bytes 120261 | solution.py:41
  248.6 0.7 dynamic_slice.42
  250.0 1.5 fusion.29
  253.0 1.5 fusion.29
  256.0 1.5 fusion.29
  258.9 1.5 fusion.29
  261.9 1.5 fusion.29
  264.9 1.5 fusion.29
  267.9 1.5 fusion.29
  270.9 1.5 fusion.29
  273.8 1.5 fusion.29
  276.8 1.5 fusion.29
  279.8 1.5 fusion.29
  282.8 1.5 fusion.29
  285.8 1.5 fusion.29
  288.7 1.5 fusion.29
  291.7 1.5 fusion.29
  294.7 1.5 fusion.29
  296.4 38.5 %psum.30 = s32[64]{0:T(128)S(1)} all-reduce(s32[64]{0:T(128)S(1)} %bitcast.29), channel_id=1, replica_groups=mesh['clients'=8,'shard'=4] {'clients','shard'}, use_global_device_ids=true, to_apply=%region_10.11 | all-reduce | flops 64 | bytes 512 | tf_op jit(solution)/shard_map/psum | solution.py:67
  (182 shorter events, 22.7 us)
Async XLA Ops:
  7.2 238.8 %all-reduce.2.cloned.1.call-start = ((), (), s32[]{:S(2)}) async-start(), calls=%async_computation | async-start | bytes 4194304 | tf_op jit(solution)/shard_map/psum | solution.py:55
  20.0 0.7 copy-start.1
  248.5 86.9 %copy-start = (s32[524288]{0:T(1024)}, s32[524288]{0:T(1024)S(1)}, u32[]{:S(2)}) copy-start(s32[524288]{0:T(1024)S(1)} %add_select_fusion.4) | copy-start | bytes 6291460
Sparse Core Ops, SparseCore 0:
  20.1 105.0 all-reduce.1
where the time goes:
time: 343 us; the launch traced here: 342 us
  other arithmetic  210 us (61%)
  blocking collectives  56.5 us (16%)
  local copies, waits for them, and re-layouts  39.6 us (12%)
  loops' own time  21.8 us (6%)
  between operations  14.8 us (4%)
    reduce_sum x32, other arithmetic, advance(): partial_value = jnp.sum(products, axis=3, dtype=jnp.int32) % modulus  188 us
    psum x1, blocking collectives, body(): projected = lax.psum(projected_part, ('clients', 'shard')) % modulus  38.5 us
    another operation x2, loops' own time, project_mod(): lax.scan(advance, running, jnp.arange(block_count, dtype=jnp.int32))  21.8 us
    dynamic_slice x32, local copies, waits for them, and re-layouts, project_mod(): lax.scan(advance, running, jnp.arange(block_count, dtype=jnp.int32))  19.4 us
    dynamic_slice x32, local copies, waits for them, and re-layouts, advance(): right_part = lax.dynamic_slice_in_dim(vectors, start_col, block_width, 1)  19.1 us
    psum x1, blocking collectives, body(): expected = lax.psum(weighted, 'clients') % modulus  11.6 us
    rem x1, other arithmetic, body(): masked = (quantized[0] + pair_masks[0]) % modulus * alive_now  10.4 us
  transfers between devices with their start and end apart: 1, of which 0 were waited for; matrix products, arithmetic and copies ran while one was open for 58% of the time, Pallas kernels for 0%

commit v1 on v0

v1 whole, which is shorter than its diff:
```python
import functools
import math

import jax
import jax.numpy as jnp
from jax import lax
from jax.experimental import pallas as pl
from jax.experimental.pallas import tpu as pltpu
from jax.sharding import PartitionSpec as P

modulus = 2097143
LANES = 128


def reduce_mod(x):
    x = (x & 2097151) + (x >> 21) * 9
    return jnp.where(x >= modulus, x - modulus, x)


def table_tile(start):
    v = start & 2147483647
    v = v ^ (v >> 15)
    v = (v * 277803737) & 2147483647
    v = v ^ (v >> 13)
    v = v * 1103515245
    v = v ^ (v >> 16)
    high = (v & 992).astype(jnp.float32).astype(jnp.bfloat16)
    low = (v & 31).astype(jnp.float32).astype(jnp.bfloat16)
    return high, low


def project_kernel(block, group, start_ref, seeds_ref, *refs):
    count = (len(refs) - 3) // 1
    vec_refs = refs[:count]
    out_ref, table_ref, base_ref = refs[count:]
    step = pl.program_id(0)
    rows = seeds_ref.shape[0]

    @pl.when(step == 0)
    def _():
        lane = lax.broadcasted_iota(jnp.int32, (rows, LANES), 1)
        base_ref[...] = (lane + start_ref[0]) * 747796405 + seeds_ref[...]
        out_ref[...] = jnp.zeros_like(out_ref)

    width = 8 * ((3 * count + 7) // 8)
    sub = lax.broadcasted_iota(jnp.int32, (width, group), 0)
    base = base_ref[...]
    total = None
    for g in range(block // group):
        for k in range(group // LANES):
            first = (step * block + (g * group + k * LANES)) * 747796405
            high, low = table_tile(base + first)
            cols = pl.ds(k * LANES, LANES)
            table_ref[g, :rows, cols] = high
            table_ref[g, rows:, cols] = low
        picked = None
        for n in range(count):
            one = jnp.broadcast_to(vec_refs[n][:, g * group : (g + 1) * group], (width, group))
            picked = one if picked is None else jnp.where(sub >= 3 * n, one, picked)
        shift = 7 * (sub % 3)
        pieces = ((picked >> shift) & 127).astype(jnp.float32).astype(jnp.bfloat16)
        part = lax.dot_general(
            table_ref[g], pieces, (((1,), (1,)), ((), ())), preferred_element_type=jnp.float32
        )
        total = part if total is None else total + part
    total = total.astype(jnp.int32)
    out_ref[...] = reduce_mod(out_ref[...] + total)


def project(row_seeds, vectors, start, block=4096, group=1024):
    rows = row_seeds.shape[0]
    length = vectors[0].shape[1]
    block = math.gcd(length, block)
    group = math.gcd(block, group)
    count = len(vectors)
    width = 8 * ((3 * count + 7) // 8)
    parts = pl.pallas_call(
        functools.partial(project_kernel, block, group),
        grid=(length // block,),
        in_specs=[
            pl.BlockSpec(memory_space=pltpu.SMEM),
            pl.BlockSpec((rows, 1), lambda i: (0, 0)),
        ]
        + [pl.BlockSpec((1, block), lambda i: (0, i))] * count,
        out_specs=pl.BlockSpec((2 * rows, width), lambda i: (0, 0)),
        out_shape=jax.ShapeDtypeStruct((2 * rows, width), jnp.int32),
        scratch_shapes=[
            pltpu.VMEM((block // group, 2 * rows, group), jnp.bfloat16),
            pltpu.VMEM((rows, LANES), jnp.int32),
        ],
        cost_estimate=pl.CostEstimate(
            flops=length * rows * 60, bytes_accessed=length * 4 * count, transcendentals=0
        ),
        name="project",
    )(start.reshape(1), row_seeds[:, None], *vectors)
    both = reduce_mod(parts[:rows] + parts[rows:])
    out = []
    for n in range(count):
        value = both[:, 3 * n + 2]
        value = reduce_mod(value * 128 + both[:, 3 * n + 1])
        value = reduce_mod(value * 128 + both[:, 3 * n])
        out.append(value)
    return out


def body(quantized, pair_masks, alive_flags, row_seeds):
    alive_now = alive_flags[0]
    length = quantized.shape[1]
    clients = lax.axis_size("clients")
    client = lax.axis_index("clients")
    rows = row_seeds.shape[0]
    masked = quantized + pair_masks
    masked = jnp.where(masked >= modulus, masked - modulus, masked)
    masked = jnp.where(masked >= modulus, masked - modulus, masked) * alive_now
    summed = lax.psum(masked[0], "clients")
    aggregate = reduce_mod(summed)
    offset = lax.axis_index("shard") * length
    own, arrived = project(row_seeds, [quantized, masked], offset)
    mine = jnp.arange(clients, dtype=jnp.int32)[:, None] == client
    left = jnp.where(mine, own[None, :], 0)
    diff = (arrived - own * alive_now)
    diff = jnp.where(diff < 0, diff + modulus, diff)
    both = lax.psum(jnp.concatenate([left, diff[None, :]], 0), ("clients", "shard"))
    commitments = reduce_mod(lax.dynamic_slice_in_dim(both, client, 1, 0))
    mismatch = reduce_mod(both[clients])
    return (aggregate, commitments, mismatch)


def solution(mesh):
    placed = (P("clients", "shard"), P("clients", "shard"), P("clients"), P())
    return jax.shard_map(
        body,
        mesh=mesh,
        in_specs=placed,
        out_specs=(P("shard"), P("clients", None), P()),
        check_vma=False,
    )
```

time: 343 us -> 265 us (0.77)
  other arithmetic: 210 us -> 12 us
  Pallas kernels: 0 us -> 127 us
  waiting for transfers between devices: 0.02 us -> 64.7 us
  local copies, waits for them, and re-layouts: 39.6 us -> 1.45 us
  loops' own time: 21.8 us -> 0 us
  blocking collectives: 56.5 us -> 44.9 us
    reduce_sum x64 -> x0, other arithmetic: 192 us -> none  [the longest x32 188 us: advance(): partial_value = jnp.sum(products, axis=3, dtype=jnp.int32) % modulus]
    pallas_call x0 -> x1, Pallas kernels: none -> 127 us  [project(): pl.pallas_call(functools.partial(project_kernel, block, group), grid=(len...]
    psum x1, waiting for transfers between devices: 0.01 us -> 64 us  [body(): summed = lax.psum(masked[0], 'clients')]
    dynamic_slice x65 -> x0, local copies, waits for them, and re-layouts: 38.5 us -> none  [the longest x32 19.4 us: project_mod(): lax.scan(advance, running, jnp.arange(block_count, dtype=jnp.int32))]
    another operation x2 -> x0, loops' own time: 21.8 us -> none  [project_mod(): lax.scan(advance, running, jnp.arange(block_count, dtype=jnp.int32))]
    psum x3 -> x1, blocking collectives: 56.5 us -> 44.9 us  [body(): lax.psum(jnp.concatenate([left, diff[None, :]], 0), ('clients', 'shard'))]
    rem x1 -> x0, other arithmetic: 10.4 us -> none  [body(): masked = (quantized[0] + pair_masks[0]) % modulus * alive_now]
    mul x34 -> x1, other arithmetic: 2.72 us -> 7.21 us  [body(): masked = jnp.where(masked >= modulus, masked - modulus, masked) * alive_now]
  transfers between devices with their start and end apart: 1 -> 1, of which waited for: 0 -> 1; matrix products, arithmetic and copies ran while one was open for 58% -> 1% of each run, Pallas kernels for 0% -> 0%
where the time goes in v1:
time: 265 us
  Pallas kernels  127 us (48%)
  waiting for transfers between devices  64.7 us (24%)
  blocking collectives  44.9 us (17%)
  between operations  14.7 us (6%)
  other arithmetic  12 us (5%)
    pallas_call x1, Pallas kernels, project(): pl.pallas_call(functools.partial(project_kernel, block, group), grid=(len...  127 us
    psum x1, waiting for transfers between devices, body(): summed = lax.psum(masked[0], 'clients')  64 us
    psum x1, blocking collectives, body(): lax.psum(jnp.concatenate([left, diff[None, :]], 0), ('clients', 'shard'))  44.9 us
    mul x1, other arithmetic, body(): masked = jnp.where(masked >= modulus, masked - modulus, masked) * alive_now  7.21 us
  transfers between devices with their start and end apart: 1, of which 1 were waited for; matrix products, arithmetic and copies ran while one was open for 1% of the time, Pallas kernels for 0%

profile of v1, /device:TPU:0, one launch (start us, length us, event | category | flops | bytes accessed | tf_op | source)
XLA Modules:
  0.0 264.8 jit_solution(16050440290647812865)
XLA Ops:
  7.8 1.3 copy.8.seeds_ref
  9.2 7.2 %fusion.refs_1_ = s32[1,524288]{1,0:T(1,128)} fusion(s32[1,524288]{1,0:T(1,128)} %refs_0_.1, s32[1,524288]{1,0:T(1,128)} %param.5, s32[]{:T(128)} %bitcast.30), kind=kLoop, calls=%fused_computation.3 | loop fusion | flops 4194304 | bytes 6291460 | tf_op jit(solution)/shard_map/mul | solution.py:114
  16.4 127.0 %project.1 = s32[128,8]{1,0:T(8,128)} custom-call(s32[1]{0:T(128)} %bitcast.2.start_ref, s32[64,1]{1,0:T(8,128)} %copy.8.seeds_ref, s32[1,524288]{1,0:T(1,128)} %refs_0_.1, s32[1,524288]{1,0:T(1,128)} %fusion.refs_1_), custom_call_target="tpu_custom_call" | custom-call | flops 2013265920 | bytes 4194304 | tf_op jit(solution)/shard_map/project/pallas_call | solution.py:77
  143.4 0.0 copy-start
  143.4 0.0 all-reduce.2.cloned.1.call-start
  143.4 0.7 all-reduce.2.cloned.1.call-update
  144.2 0.1 copy-done
  144.3 0.2 add_reduce_fusion
  144.6 0.1 broadcast_select_fusion
  144.6 44.9 %psum.15 = s32[9,64]{1,0:T(8,128)S(1)} all-reduce(s32[9,64]{1,0:T(8,128)S(1)} %pad_add_fusion), channel_id=1, replica_groups=mesh['clients'=8,'shard'=4] {'clients','shard'}, use_global_device_ids=true, to_apply=%region_1.2 | all-reduce | flops 576 | bytes 4608 | tf_op jit(solution)/shard_map/psum | solution.py:123
  189.5 0.5 compare_select_fusion.5
  190.0 0.5 compare_select_fusion.4
  190.5 64.0 %all-reduce.2.cloned.1.call-done = s32[524288]{0:T(1024)} async-done(((s32[524288]{0:T(1024)}), s32[524288]{0:T(1024)}) %all-reduce.2.cloned.1.call-update) | async-done | bytes 2097168 | tf_op jit(solution)/shard_map/psum | solution.py:115
  254.6 3.4 %compare_select_fusion.2 = s32[524288]{0:T(1024)} fusion(s32[524288]{0:T(1024)} %all-reduce.2.cloned.1.call-done), kind=kLoop, calls=%fused_computation.2 | loop fusion | flops 3670016 | bytes 4194304 | tf_op jit(solution)/shard_map/jit(_where)/select_n | solution.py:17
  (5 shorter events, 0.1 us)
Async XLA Ops:
  143.4 0.8 copy-start
  143.4 111.1 %all-reduce.2.cloned.1.call-start = ((), (), s32[]{:S(2)}) async-start(), calls=%async_computation | async-start | bytes 4194304 | tf_op jit(solution)/shard_map/psum | solution.py:115
Sparse Core Ops, SparseCore 0:
  148.4 106.0 all-reduce.1

commit v2 on v1

v2 whole, which is shorter than its diff:
```python
import functools

import jax
import jax.numpy as jnp
from jax import lax
from jax.experimental import pallas as pl
from jax.experimental.pallas import tpu as pltpu
from jax.sharding import PartitionSpec as P

modulus = 2097143
LANES = 128
GROUP = 16
STRIDE = (LANES * 747796405 + 2147483648) % 4294967296 - 2147483648


def reduce_mod(x):
    x = (x & 2097151) + (x >> 21) * 9
    return jnp.where(x >= modulus, x - modulus, x)


def table_tile(start):
    v = start & 2147483647
    v = v ^ (v >> 15)
    v = (v * 277803737) & 2147483647
    v = v ^ (v >> 13)
    v = v * 1103515245
    v = v ^ (v >> 16)
    high = (v & 992).astype(jnp.float32).astype(jnp.bfloat16)
    low = (v & 31).astype(jnp.float32).astype(jnp.bfloat16)
    return high, low


def aggregate_kernel(
    clients,
    length,
    alive_ref,
    seeds_ref,
    quant_ref,
    masks_ref,
    agg_out,
    proj_out,
    masked,
    arrived,
    agg,
    base,
    tables,
    pieces,
    send_sem,
    recv_sem,
    out_sem,
):
    rows = quant_ref.shape[0]
    half = rows // 2
    checks = seeds_ref.shape[0]
    bits = clients.bit_length() - 1
    me = lax.axis_index("clients")
    start = lax.axis_index("shard") * length
    alive = alive_ref[0]

    barrier = pltpu.get_barrier_semaphore()
    for b in range(bits):
        pl.semaphore_signal(barrier, inc=1, device_id={"clients": me ^ (1 << b)})

    def mask_rows(lo, count):
        step = min(64, count)

        @pl.loop(0, count // step)
        def _(i):
            at = pl.ds(pl.multiple_of(lo + i * step, 8), step)
            s = quant_ref[at, :] + masks_ref[at, :]
            s = jnp.where(s >= modulus, s - modulus, s)
            s = jnp.where(s >= modulus, s - modulus, s)
            masked[at, :] = s * alive

    plans = []
    for h in range(2):
        order = list(range(bits))
        if h == 1:
            order = order[1:] + order[:1]
        lo = h * half
        count = half
        landing = h * half
        scatter, gather = [], []
        for n, b in enumerate(order):
            count //= 2
            bit = (me >> b) & 1
            keep = pl.multiple_of(lo + bit * count, 8)
            give = pl.multiple_of(lo + (1 - bit) * count, 8)
            scatter.append((b, keep, give, count, landing, n))
            gather.append((b, keep, give, count, n))
            landing += count
            lo = keep
        plans.append((scatter, gather[::-1], lo, count))

    def scatter_copy(h, n):
        b, keep, give, count, landing, _ = plans[h][0][n]
        return pltpu.make_async_remote_copy(
            src_ref=masked.at[pl.ds(give, count)],
            dst_ref=arrived.at[pl.ds(landing, count)],
            send_sem=send_sem.at[h, n],
            recv_sem=recv_sem.at[h, n],
            device_id={"clients": me ^ (1 << b)},
        )

    def gather_copy(h, n):
        b, keep, give, count, _ = plans[h][1][n]
        return pltpu.make_async_remote_copy(
            src_ref=agg.at[pl.ds(keep, count)],
            dst_ref=agg.at[pl.ds(keep, count)],
            send_sem=send_sem.at[h, bits + n],
            recv_sem=recv_sem.at[h, bits + n],
            device_id={"clients": me ^ (1 << b)},
        )

    def gather_wait(h, n):
        b, keep, give, count, _ = plans[h][1][n]
        gather_copy(h, n).wait_send()
        pltpu.make_async_remote_copy(
            src_ref=agg.at[pl.ds(give, count)],
            dst_ref=agg.at[pl.ds(give, count)],
            send_sem=send_sem.at[h, bits + n],
            recv_sem=recv_sem.at[h, bits + n],
            device_id={"clients": me ^ (1 << b)},
        ).wait_recv()

    def add_arrived(h, n):
        _, keep, _, count, landing, _ = plans[h][0][n]
        step = min(64, count)
        last = n == bits - 1

        @pl.loop(0, count // step)
        def _(i):
            at = pl.ds(pl.multiple_of(keep + i * step, 8), step)
            got = pl.ds(pl.multiple_of(landing + i * step, 8), step)
            s = masked[at, :] + arrived[got, :]
            if last:
                agg[at, :] = reduce_mod(s)
            else:
                masked[at, :] = s

    for h in range(2):
        _, keep, give, count, _, _ = plans[h][0][0]
        mask_rows(give, count)
    lane = lax.broadcasted_iota(jnp.int32, (checks, LANES), 1)
    base[...] = (lane + start) * 747796405 + seeds_ref[...]
    tables[1] = jnp.zeros_like(tables[1])
    pieces[1] = jnp.zeros_like(pieces[1])
    pl.semaphore_wait(barrier, bits)
    for h in range(2):
        scatter_copy(h, 0).start()
    for h in range(2):
        _, keep, give, count, _, _ = plans[h][0][0]
        mask_rows(keep, count)

    sub = lax.broadcasted_iota(jnp.int32, (8, LANES), 0)
    shift = 7 * (sub & 3)
    second = sub >= 4

    def pending(slot, total):
        part = lax.dot_general(
            pieces[slot], tables[slot], (((1,), (1,)), ((), ())), preferred_element_type=jnp.float32
        )
        return reduce_mod(total + part.astype(jnp.int32))

    def fill(slot, row):
        for k in range(GROUP):
            at = row + k
            high, low = table_tile(base[...] + at * STRIDE)
            cols = pl.ds(k * LANES, LANES)
            tables[slot, :checks, cols] = high
            tables[slot, checks:, cols] = low
            one = jnp.broadcast_to(quant_ref[pl.ds(at, 1), :], (8, LANES))
            two = jnp.broadcast_to(masked_row(at), (8, LANES))
            both = (jnp.where(second, two, one) >> shift) & 127
            pieces[slot, :, cols] = both.astype(jnp.float32).astype(jnp.bfloat16)

    def masked_row(at):
        s = quant_ref[pl.ds(at, 1), :] + masks_ref[pl.ds(at, 1), :]
        s = jnp.where(s >= modulus, s - modulus, s)
        return jnp.where(s >= modulus, s - modulus, s) * alive

    def compute(first, count, total):
        def pair(i, total):
            row = first + i * (2 * GROUP)
            total = pending(1, total)
            fill(0, row)
            total = pending(0, total)
            fill(1, row + GROUP)
            return total

        return lax.fori_loop(0, count, pair, total)

    actions = []
    for n in range(bits):
        for h in range(2):
            def take(h=h, n=n):
                scatter_copy(h, n).wait()
                add_arrived(h, n)

            def send(h=h, n=n):
                if n < bits - 1:
                    scatter_copy(h, n + 1).start()
                else:
                    gather_copy(h, 0).start()

            actions.append((take, send))
    for n in range(bits):
        for h in range(2):
            def take(h=h, n=n):
                gather_wait(h, n)

            def send(h=h, n=n):
                if n < bits - 1:
                    gather_copy(h, n + 1).start()

            actions.append((take, send))

    pairs = rows // (2 * GROUP)
    stops = len(actions) + 1
    done = 0
    total = jnp.zeros((8, LANES), jnp.int32)
    for s, (take, send) in enumerate(actions):
        until = pairs * (s + 1) // stops
        total = compute(done * 2 * GROUP, until - done, total)
        done = until
        take()
        send()
    store = pltpu.make_async_copy(agg, agg_out, out_sem)
    store.start()
    total = compute(done * 2 * GROUP, pairs - done, total)
    proj_out[...] = pending(1, total)
    store.wait()


def aggregate_and_project(quantized, pair_masks, alive_flags, row_seeds, clients):
    length = quantized.shape[1]
    rows = length // LANES
    checks = row_seeds.shape[0]
    bits = clients.bit_length() - 1
    vmem = pl.BlockSpec(memory_space=pltpu.VMEM)
    return pl.pallas_call(
        functools.partial(aggregate_kernel, clients, length),
        in_specs=[pl.BlockSpec(memory_space=pltpu.SMEM), vmem, vmem, vmem],
        out_specs=[pl.BlockSpec(memory_space=pl.ANY), vmem],
        out_shape=[
            jax.ShapeDtypeStruct((rows, LANES), jnp.int32),
            jax.ShapeDtypeStruct((8, 2 * checks), jnp.int32),
        ],
        scratch_shapes=[
            pltpu.VMEM((rows, LANES), jnp.int32),
            pltpu.VMEM((rows, LANES), jnp.int32),
            pltpu.VMEM((rows, LANES), jnp.int32),
            pltpu.VMEM((checks, LANES), jnp.int32),
            pltpu.VMEM((2, 2 * checks, GROUP * LANES), jnp.bfloat16),
            pltpu.VMEM((2, 8, GROUP * LANES), jnp.bfloat16),
            pltpu.SemaphoreType.DMA((2, 2 * bits)),
            pltpu.SemaphoreType.DMA((2, 2 * bits)),
            pltpu.SemaphoreType.DMA,
        ],
        compiler_params=pltpu.CompilerParams(collective_id=0, has_side_effects=True),
        name="aggregate_and_project",
    )(
        alive_flags,
        row_seeds[:, None],
        quantized.reshape(rows, LANES),
        pair_masks.reshape(rows, LANES),
    )


def body(quantized, pair_masks, alive_flags, row_seeds):
    alive_now = alive_flags[0]
    length = quantized.shape[1]
    clients = lax.axis_size("clients")
    client = lax.axis_index("clients")
    checks = row_seeds.shape[0]
    aggregate, parts = aggregate_and_project(
        quantized, pair_masks, alive_flags, row_seeds, clients
    )
    parts = reduce_mod(parts[:, :checks] + parts[:, checks:])
    own, arrived = [
        reduce_mod(reduce_mod(parts[n + 2] * 128 + parts[n + 1]) * 128 + parts[n]) for n in (0, 4)
    ]
    mine = jnp.arange(clients, dtype=jnp.int32)[:, None] == client
    left = jnp.where(mine, own[None, :], 0)
    diff = arrived - own * alive_now
    diff = jnp.where(diff < 0, diff + modulus, diff)
    both = lax.psum(jnp.concatenate([left, diff[None, :]], 0), ("clients", "shard"))
    commitments = reduce_mod(lax.dynamic_slice_in_dim(both, client, 1, 0))
    mismatch = reduce_mod(both[clients])
    return (aggregate.reshape(length), commitments, mismatch)


def solution(mesh):
    placed = (P("clients", "shard"), P("clients", "shard"), P("clients"), P())
    return jax.shard_map(
        body,
        mesh=mesh,
        in_specs=placed,
        out_specs=(P("shard"), P("clients", None), P()),
        check_vma=False,
    )
```

time: 265 us -> 179 us (0.68)
  waiting for transfers between devices: 64.7 us -> 0 us
  between operations: 14.7 us -> 1.3 us
  other arithmetic: 12 us -> 1.99 us
  blocking collectives: 44.9 us -> 39.3 us
  Pallas kernels: 127 us -> 132 us
  local copies, waits for them, and re-layouts: 1.45 us -> 4.4 us
    psum x1 -> x0, waiting for transfers between devices: 64 us -> none  [body(): summed = lax.psum(masked[0], 'clients')]
    mul x1 -> x0, other arithmetic: 7.21 us -> none  [body(): masked = jnp.where(masked >= modulus, masked - modulus, masked) * alive_now]
    psum x1, blocking collectives: 44.9 us -> 39.3 us  [body(): lax.psum(jnp.concatenate([left, diff[None, :]], 0), ('clients', 'shard'))]
    pallas_call x1, Pallas kernels: 127 us -> 132 us  [aggregate_and_project(): pl.pallas_call(functools.partial(aggregate_kernel, clients, length), in_s...]
    unnamed x2 -> x1, local copies, waits for them, and re-layouts: 0.1 us -> 3.04 us
  transfers between devices with their start and end apart: 1 -> 0, of which waited for: 1 -> 0; matrix products, arithmetic and copies ran while one was open for 1% -> 0% of each run, Pallas kernels for 0% -> 0%
where the time goes in v2:
time: 179 us
  Pallas kernels  132 us (74%)
  blocking collectives  39.3 us (22%)
  local copies, waits for them, and re-layouts  4.4 us (2%)
  other arithmetic  1.99 us (1%)
    pallas_call x1, Pallas kernels, aggregate_and_project(): pl.pallas_call(functools.partial(aggregate_kernel, clients, length), in_s...  132 us
    psum x1, blocking collectives, body(): lax.psum(jnp.concatenate([left, diff[None, :]], 0), ('clients', 'shard'))  39.3 us

profile of v2, /device:TPU:0, one launch (start us, length us, event | category | flops | bytes accessed | tf_op | source)
XLA Modules:
  0.0 178.9 jit_solution(15357528380356236883)
XLA Ops:
  1.3 1.4 copy.7.seeds_ref
  2.6 131.9 %aggregate_and_project.1 = (s32[4096,128]{1,0:T(8,128)}, s32[8,128]{1,0:T(8,128)}) custom-call(s32[1]{0:T(128)} %copy.9.alive_ref, s32[64,1]{1,0:T(8,128)} %copy.7.seeds_ref, s32[4096,128]{1,0:T(8,128)} %bitcast.9, s32[4096,128]{1,0:T(8,128)} %bitcast.10), custom_call_target="tpu_custom_call" | custom-call | tf_op jit(solution)/shard_map/aggregate_and_project/pallas_call | solution.py:241
  134.5 0.8 compare_select_fusion
  135.4 0.1 broadcast_select_fusion
  135.5 39.3 %psum.7 = s32[9,64]{1,0:T(8,128)S(1)} all-reduce(s32[9,64]{1,0:T(8,128)S(1)} %pad_add_fusion), channel_id=1, replica_groups=mesh['clients'=8,'shard'=4] {'clients','shard'}, use_global_device_ids=true, to_apply=%region_0.1 | all-reduce | flops 576 | bytes 4608 | tf_op jit(solution)/shard_map/psum | solution.py:287
  174.8 0.5 compare_select_fusion.2
  175.4 0.5 compare_select_fusion.1
  175.9 3.0 %copy.10 = s32[524288]{0:T(1024)} copy(s32[524288]{0:T(1024)} %bitcast.11) | data formatting | bytes 4194304
  (3 shorter events, 0.0 us)

commit v3 on v2

--- a/solution.py
+++ b/solution.py
@@ -38,7 +38,8 @@
     quant_ref,
     masks_ref,
     agg_out,
-    proj_out,
+    own_out,
+    diff_out,
     masked,
     arrived,
     agg,
@@ -48,18 +49,28 @@
     send_sem,
     recv_sem,
     out_sem,
+    own_parts,
+    diff_parts,
+    own_send,
+    own_recv,
+    diff_send,
+    diff_recv,
 ):
     rows = quant_ref.shape[0]
     half = rows // 2
     checks = seeds_ref.shape[0]
     bits = clients.bit_length() - 1
     me = lax.axis_index("clients")
+    shards = lax.axis_size("shard")
+    here = lax.axis_index("shard")
     start = lax.axis_index("shard") * length
     alive = alive_ref[0]
 
     barrier = pltpu.get_barrier_semaphore()
-    for b in range(bits):
-        pl.semaphore_signal(barrier, inc=1, device_id={"clients": me ^ (1 << b)})
+    for n in range(1, clients):
+        pl.semaphore_signal(barrier, inc=1, device_id={"clients": me ^ n})
+    for n in range(1, shards):
+        pl.semaphore_signal(barrier, inc=1, device_id={"shard": lax.rem(here + n, shards)})
 
     def mask_rows(lo, count):
         step = min(64, count)
@@ -145,7 +156,7 @@
     base[...] = (lane + start) * 747796405 + seeds_ref[...]
     tables[1] = jnp.zeros_like(tables[1])
     pieces[1] = jnp.zeros_like(pieces[1])
-    pl.semaphore_wait(barrier, bits)
+    pl.semaphore_wait(barrier, clients + shards - 2)
     for h in range(2):
         scatter_copy(h, 0).start()
     for h in range(2):
@@ -228,11 +239,51 @@
     store = pltpu.make_async_copy(agg, agg_out, out_sem)
     store.start()
     total = compute(done * 2 * GROUP, pairs - done, total)
-    proj_out[...] = pending(1, total)
+    total = pending(1, total)
+
+    own_parts[0] = total
+    own_copies = [
+        pltpu.make_async_remote_copy(
+            src_ref=own_parts.at[0],
+            dst_ref=own_parts.at[n],
+            send_sem=own_send.at[n],
+            recv_sem=own_recv.at[n],
+            device_id={"shard": lax.rem(here + n, shards)},
+        )
+        for n in range(1, shards)
+    ]
+    for copy in own_copies:
+        copy.start()
+    for copy in own_copies:
+        copy.wait()
+    for n in range(1, shards):
+        total = total + own_parts[n]
+    total = reduce_mod(total)
+    own_out[...] = total
+    diff = pltpu.roll(total, 4, 0) - total * alive
+    diff = jnp.where(diff < 0, diff + modulus, diff)
+    diff_parts[0] = diff
+    diff_copies = [
+        pltpu.make_async_remote_copy(
+            src_ref=diff_parts.at[0],
+            dst_ref=diff_parts.at[n],
+            send_sem=diff_send.at[n],
+            recv_sem=diff_recv.at[n],
+            device_id={"clients": me ^ n},
+        )
+        for n in range(1, clients)
+    ]
+    for copy in diff_copies:
+        copy.start()
+    for copy in diff_copies:
+        copy.wait()
+    for n in range(1, clients):
+        diff = diff + diff_parts[n]
+    diff_out[...] = reduce_mod(diff)
     store.wait()
 
 
-def aggregate_and_project(quantized, pair_masks, alive_flags, row_seeds, clients):
+def aggregate_and_project(quantized, pair_masks, alive_flags, row_seeds, clients, shards):
     length = quantized.shape[1]
     rows = length // LANES
     checks = row_seeds.shape[0]
@@ -241,9 +292,10 @@
     return pl.pallas_call(
         functools.partial(aggregate_kernel, clients, length),
         in_specs=[pl.BlockSpec(memory_space=pltpu.SMEM), vmem, vmem, vmem],
-        out_specs=[pl.BlockSpec(memory_space=pl.ANY), vmem],
+        out_specs=[pl.BlockSpec(memory_space=pl.ANY), vmem, vmem],
         out_shape=[
             jax.ShapeDtypeStruct((rows, LANES), jnp.int32),
+            jax.ShapeDtypeStruct((8, 2 * checks), jnp.int32),
             jax.ShapeDtypeStruct((8, 2 * checks), jnp.int32),
         ],
         scratch_shapes=[
@@ -256,6 +308,12 @@
             pltpu.SemaphoreType.DMA((2, 2 * bits)),
             pltpu.SemaphoreType.DMA((2, 2 * bits)),
             pltpu.SemaphoreType.DMA,
+            pltpu.VMEM((shards, 8, 2 * checks), jnp.int32),
+            pltpu.VMEM((clients, 8, 2 * checks), jnp.int32),
+            pltpu.SemaphoreType.DMA((shards,)),
+            pltpu.SemaphoreType.DMA((shards,)),
+            pltpu.SemaphoreType.DMA((clients,)),
+            pltpu.SemaphoreType.DMA((clients,)),
         ],
         compiler_params=pltpu.CompilerParams(collective_id=0, has_side_effects=True),
         name="aggregate_and_project",
@@ -267,27 +325,20 @@
     )
 
 
+def checksum(parts):
+    checks = parts.shape[1] // 2
+    parts = reduce_mod(parts[:, :checks] + parts[:, checks:])
+    return reduce_mod(reduce_mod(parts[2] * 128 + parts[1]) * 128 + parts[0])
+
+
 def body(quantized, pair_masks, alive_flags, row_seeds):
-    alive_now = alive_flags[0]
     length = quantized.shape[1]
     clients = lax.axis_size("clients")
-    client = lax.axis_index("clients")
-    checks = row_seeds.shape[0]
-    aggregate, parts = aggregate_and_project(
-        quantized, pair_masks, alive_flags, row_seeds, clients
+    shards = lax.axis_size("shard")
+    aggregate, own, diff = aggregate_and_project(
+        quantized, pair_masks, alive_flags, row_seeds, clients, shards
     )
-    parts = reduce_mod(parts[:, :checks] + parts[:, checks:])
-    own, arrived = [
-        reduce_mod(reduce_mod(parts[n + 2] * 128 + parts[n + 1]) * 128 + parts[n]) for n in (0, 4)
-    ]
-    mine = jnp.arange(clients, dtype=jnp.int32)[:, None] == client
-    left = jnp.where(mine, own[None, :], 0)
-    diff = arrived - own * alive_now
-    diff = jnp.where(diff < 0, diff + modulus, diff)
-    both = lax.psum(jnp.concatenate([left, diff[None, :]], 0), ("clients", "shard"))
-    commitments = reduce_mod(lax.dynamic_slice_in_dim(both, client, 1, 0))
-    mismatch = reduce_mod(both[clients])
-    return (aggregate.reshape(length), commitments, mismatch)
+    return (aggregate.reshape(length), checksum(own)[None, :], checksum(diff))
 
 
 def solution(mesh):

time: 179 us -> 147 us (0.82)
  blocking collectives: 39.3 us -> 0 us
  Pallas kernels: 132 us -> 140 us
    psum x1 -> x0, blocking collectives: 39.3 us -> none  [body(): lax.psum(jnp.concatenate([left, diff[None, :]], 0), ('clients', 'shard'))]
    pallas_call x1, Pallas kernels: 132 us -> 140 us  [aggregate_and_project(): pl.pallas_call(functools.partial(aggregate_kernel, clients, length), in_s...]
where the time goes in v3:
time: 147 us
  Pallas kernels  140 us (95%)
  local copies, waits for them, and re-layouts  4.4 us (3%)
  other arithmetic  1.89 us (1%)
    pallas_call x1, Pallas kernels, aggregate_and_project(): pl.pallas_call(functools.partial(aggregate_kernel, clients, length), in_s...  140 us
    unnamed x1, local copies, waits for them, and re-layouts  3.04 us

profile of v3, /device:TPU:0, one launch (start us, length us, event | category | flops | bytes accessed | tf_op | source)
XLA Modules:
  0.0 147.1 jit_solution(12555302346559820421)
XLA Ops:
  0.6 1.4 copy.7.seeds_ref
  2.6 139.5 %aggregate_and_project.1 = (s32[4096,128]{1,0:T(8,128)}, s32[8,128]{1,0:T(8,128)}, s32[8,128]{1,0:T(8,128)}) custom-call(s32[1]{0:T(128)S(6)} %copy.9.alive_ref, s32[64,1]{1,0:T(8,128)} %copy.7.seeds_ref, s32[4096,128]{1,0:T(8,128)} %bitcast.12, s32[4096,128]{1,0:T(8,128)} %bitcast.13), custom_call_target="tpu_custom_call" | custom-call | tf_op jit(solution)/shard_map/aggregate_and_project/pallas_call | solution.py:292
  142.2 0.8 compare_select_fusion
  143.0 0.5 compare_select_fusion.2
  143.6 0.5 compare_select_fusion.4
  144.1 3.0 %copy.10 = s32[524288]{0:T(1024)} copy(s32[524288]{0:T(1024)} %bitcast.14) | data formatting | bytes 4194304

commit v4 on v3

--- a/solution.py
+++ b/solution.py
@@ -55,6 +55,9 @@
     own_recv,
     diff_send,
     diff_recv,
+    partner_q,
+    swap_send,
+    swap_recv,
 ):
     rows = quant_ref.shape[0]
     half = rows // 2
@@ -70,7 +73,10 @@
     for n in range(1, clients):
         pl.semaphore_signal(barrier, inc=1, device_id={"clients": me ^ n})
     for n in range(1, shards):
-        pl.semaphore_signal(barrier, inc=1, device_id={"shard": lax.rem(here + n, shards)})
+        there = lax.rem(here + n, shards)
+        pl.semaphore_signal(barrier, inc=1, device_id={"shard": there})
+        pl.semaphore_signal(barrier, inc=1, device_id={"shard": there, "clients": me ^ 1})
+    peers = clients + 2 * shards - 3
 
     def mask_rows(lo, count):
         step = min(64, count)
@@ -149,21 +155,72 @@
             else:
                 masked[at, :] = s
 
-    for h in range(2):
+    block = half // clients
+    shares = [plans[0][2] // block, (plans[1][2] - half) // block]
+    unit = 2 * GROUP
+    per_block = block // unit
+    others = clients // 2 - 1
+
+    def block_row(h, k, flip=0):
+        if h == 0:
+            return (shares[0] ^ (k + flip * (clients // 2))) * block
+        return half + (shares[1] ^ (2 * k + flip)) * block
+
+    work = [(h, k) for h in range(2) for k in range(others, 0, -1)] + [(0, 0), (1, 0)]
+
+    def swap_copy(n):
+        at = pl.multiple_of(block_row(*work[n], 1), 8)
+        return pltpu.make_async_remote_copy(
+            src_ref=quant_ref.at[pl.ds(at, block)],
+            dst_ref=partner_q.at[pl.ds(at, block)],
+            send_sem=swap_send.at[n],
+            recv_sem=swap_recv.at[n],
+            device_id={"clients": me ^ 1},
+        )
+
+    def swap_wait(n):
+        swap_copy(n).wait_send()
+        at = pl.multiple_of(block_row(*work[n]), 8)
+        pltpu.make_async_remote_copy(
+            src_ref=partner_q.at[pl.ds(at, block)],
+            dst_ref=partner_q.at[pl.ds(at, block)],
+            send_sem=swap_send.at[n],
+            recv_sem=swap_recv.at[n],
+            device_id={"clients": me ^ 1},
+        ).wait_recv()
+
+    def pair_row(u, share):
+        each = per_block if share else others * per_block
+        r = u - (0 if not share else 2 * others * per_block)
+        h = (r >= each).astype(jnp.int32)
+        r = r - h * each
+        k = 0 if share else others - r // per_block
+        a = (shares[0] ^ k) * block
+        b = half + (shares[1] ^ (2 * k)) * block
+        row = jnp.where(h == 1, b, a) + (r % per_block) * unit
+        return pl.multiple_of(row, unit)
+
+    early = min(2, len(work))
+    pl.semaphore_wait(barrier, peers)
+    for n in range(early):
+        swap_copy(n).start()
+    for h in (1, 0):
         _, keep, give, count, _, _ = plans[h][0][0]
         mask_rows(give, count)
     lane = lax.broadcasted_iota(jnp.int32, (checks, LANES), 1)
     base[...] = (lane + start) * 747796405 + seeds_ref[...]
     tables[1] = jnp.zeros_like(tables[1])
     pieces[1] = jnp.zeros_like(pieces[1])
-    pl.semaphore_wait(barrier, clients + shards - 2)
-    for h in range(2):
+    for h in (1, 0):
         scatter_copy(h, 0).start()
+    for n in range(early, len(work)):
+        swap_copy(n).start()
     for h in range(2):
         _, keep, give, count, _, _ = plans[h][0][0]
         mask_rows(keep, count)
 
     sub = lax.broadcasted_iota(jnp.int32, (8, LANES), 0)
+    empty = jnp.zeros((8, LANES), jnp.float32)
     shift = 7 * (sub & 3)
     second = sub >= 4
 
@@ -173,7 +230,7 @@
         )
         return reduce_mod(total + part.astype(jnp.int32))
 
-    def fill(slot, row):
+    def fill(slot, row, share):
         for k in range(GROUP):
             at = row + k
             high, low = table_tile(base[...] + at * STRIDE)
@@ -181,29 +238,30 @@
             tables[slot, :checks, cols] = high
             tables[slot, checks:, cols] = low
             one = jnp.broadcast_to(quant_ref[pl.ds(at, 1), :], (8, LANES))
-            two = jnp.broadcast_to(masked_row(at), (8, LANES))
-            both = (jnp.where(second, two, one) >> shift) & 127
-            pieces[slot, :, cols] = both.astype(jnp.float32).astype(jnp.bfloat16)
-
-    def masked_row(at):
-        s = quant_ref[pl.ds(at, 1), :] + masks_ref[pl.ds(at, 1), :]
-        s = jnp.where(s >= modulus, s - modulus, s)
-        return jnp.where(s >= modulus, s - modulus, s) * alive
-
-    def compute(first, count, total):
-        def pair(i, total):
-            row = first + i * (2 * GROUP)
+            two = jnp.broadcast_to(partner_q[pl.ds(at, 1), :], (8, LANES))
+            both = ((jnp.where(second, two, one) >> shift) & 127).astype(jnp.float32)
+            if share:
+                three = jnp.broadcast_to(agg[pl.ds(at, 1), :], (8, LANES))
+                third = jnp.where(second, 0, (three >> shift) & 127).astype(jnp.float32)
+            else:
+                third = empty
+            both = jnp.concatenate([both, third], 0)
+            pieces[slot, :, cols] = both.astype(jnp.bfloat16)
+
+    def compute(first, last, share, total):
+        def pair(u, total):
+            row = pair_row(u, share)
             total = pending(1, total)
-            fill(0, row)
+            fill(0, row, share)
             total = pending(0, total)
-            fill(1, row + GROUP)
+            fill(1, row + GROUP, share)
             return total
 
-        return lax.fori_loop(0, count, pair, total)
+        return lax.fori_loop(first, last, pair, total)
 
     actions = []
     for n in range(bits):
-        for h in range(2):
+        for h in (1, 0):
             def take(h=h, n=n):
                 scatter_copy(h, n).wait()
                 add_arrived(h, n)
@@ -216,7 +274,7 @@
 
             actions.append((take, send))
     for n in range(bits):
-        for h in range(2):
+        for h in (1, 0):
             def take(h=h, n=n):
                 gather_wait(h, n)
 
@@ -226,41 +284,56 @@
 
             actions.append((take, send))
 
-    pairs = rows // (2 * GROUP)
-    stops = len(actions) + 1
-    done = 0
-    total = jnp.zeros((8, LANES), jnp.int32)
-    for s, (take, send) in enumerate(actions):
-        until = pairs * (s + 1) // stops
-        total = compute(done * 2 * GROUP, until - done, total)
+    pairs = rows // 2 // unit
+    shared_from = 2 * others * per_block
+    early_part = pairs * 11 // 16
+    stops = [early_part * (i + 1) // (2 * bits) for i in range(2 * bits)]
+    stops += [
+        early_part + (pairs - early_part) * (i + 1) // (2 * bits) for i in range(2 * bits)
+    ]
+    done, swapped = 0, 0
+    total = jnp.zeros((16, LANES), jnp.int32)
+    for until, (take, send) in zip(stops, actions):
+        while swapped * per_block < until:
+            swap_wait(swapped)
+            swapped += 1
+        if done < min(until, shared_from):
+            total = compute(done, min(until, shared_from), False, total)
+        if max(done, shared_from) < until:
+            total = compute(max(done, shared_from), until, True, total)
         done = until
         take()
         send()
     store = pltpu.make_async_copy(agg, agg_out, out_sem)
     store.start()
-    total = compute(done * 2 * GROUP, pairs - done, total)
     total = pending(1, total)
 
     own_parts[0] = total
-    own_copies = [
-        pltpu.make_async_remote_copy(
-            src_ref=own_parts.at[0],
-            dst_ref=own_parts.at[n],
-            send_sem=own_send.at[n],
-            recv_sem=own_recv.at[n],
-            device_id={"shard": lax.rem(here + n, shards)},
-        )
-        for n in range(1, shards)
-    ]
+    own_copies = []
+    for n in range(1, 2 * shards):
+        where = {"shard": lax.rem(here + n % shards, shards)} if n % shards else {}
+        if n >= shards:
+            where["clients"] = me ^ 1
+        own_copies.append(
+            pltpu.make_async_remote_copy(
+                src_ref=own_parts.at[0],
+                dst_ref=own_parts.at[n],
+                send_sem=own_send.at[n],
+                recv_sem=own_recv.at[n],
+                device_id=where,
+            )
+        )
     for copy in own_copies:
         copy.start()
     for copy in own_copies:
         copy.wait()
+    mine, theirs = own_parts[0], own_parts[shards]
     for n in range(1, shards):
-        total = total + own_parts[n]
-    total = reduce_mod(total)
+        mine = mine + own_parts[n]
+        theirs = theirs + own_parts[shards + n]
+    total = reduce_mod(mine[:8] + pltpu.roll(theirs[:8], 4, 0))
     own_out[...] = total
-    diff = pltpu.roll(total, 4, 0) - total * alive
+    diff = reduce_mod(mine[8:]) - total * alive
     diff = jnp.where(diff < 0, diff + modulus, diff)
     diff_parts[0] = diff
     diff_copies = [
@@ -304,14 +377,17 @@
             pltpu.VMEM((rows, LANES), jnp.int32),
             pltpu.VMEM((checks, LANES), jnp.int32),
             pltpu.VMEM((2, 2 * checks, GROUP * LANES), jnp.bfloat16),
-            pltpu.VMEM((2, 8, GROUP * LANES), jnp.bfloat16),
+            pltpu.VMEM((2, 16, GROUP * LANES), jnp.bfloat16),
             pltpu.SemaphoreType.DMA((2, 2 * bits)),
             pltpu.SemaphoreType.DMA((2, 2 * bits)),
             pltpu.SemaphoreType.DMA,
-            pltpu.VMEM((shards, 8, 2 * checks), jnp.int32),
+            pltpu.VMEM((2 * shards, 16, 2 * checks), jnp.int32),
             pltpu.VMEM((clients, 8, 2 * checks), jnp.int32),
-            pltpu.SemaphoreType.DMA((shards,)),
-            pltpu.SemaphoreType.DMA((shards,)),
+            pltpu.SemaphoreType.DMA((2 * shards,)),
+            pltpu.SemaphoreType.DMA((2 * shards,)),
+            pltpu.SemaphoreType.DMA((clients,)),
+            pltpu.SemaphoreType.DMA((clients,)),
+            pltpu.VMEM((rows, LANES), jnp.int32),
             pltpu.SemaphoreType.DMA((clients,)),
             pltpu.SemaphoreType.DMA((clients,)),
         ],

time: 147 us -> 109 us (0.74)
  Pallas kernels: 140 us -> 101 us
    pallas_call x1, Pallas kernels: 140 us -> 101 us  [aggregate_and_project(): pl.pallas_call(functools.partial(aggregate_kernel, clients, length), in_s...]
where the time goes in v4:
time: 109 us
  Pallas kernels  101 us (93%)
  local copies, waits for them, and re-layouts  4.4 us (4%)
  other arithmetic  1.89 us (2%)
  between operations  1.29 us (1%)
    pallas_call x1, Pallas kernels, aggregate_and_project(): pl.pallas_call(functools.partial(aggregate_kernel, clients, length), in_s...  101 us
    unnamed x1, local copies, waits for them, and re-layouts  3.04 us

profile of v4, /device:TPU:0, one launch (start us, length us, event | category | flops | bytes accessed | tf_op | source)
XLA Modules:
  0.0 108.8 jit_solution(776859188835170135)
XLA Ops:
  0.6 1.4 %copy.7.seeds_ref = s32[64,1]{1,0:T(8,128)} copy(s32[64,1]{0,1:T(1,128)} %bitcast.15) | data formatting | bytes 512 | tf_op jit(solution)/shard_map/broadcast_in_dim | solution.py:398
  2.6 101.3 %aggregate_and_project.1 = (s32[4096,128]{1,0:T(8,128)}, s32[8,128]{1,0:T(8,128)}, s32[8,128]{1,0:T(8,128)}) custom-call(s32[1]{0:T(128)S(6)} %copy.9.alive_ref, s32[64,1]{1,0:T(8,128)} %copy.7.seeds_ref, s32[4096,128]{1,0:T(8,128)} %bitcast.12, s32[4096,128]{1,0:T(8,128)} %bitcast.13), custom_call_target="tpu_custom_call" | custom-call | tf_op jit(solution)/shard_map/aggregate_and_project/pallas_call | solution.py:365
  103.9 0.8 compare_select_fusion
  104.7 0.5 compare_select_fusion.2
  105.3 0.5 compare_select_fusion.4
  105.8 3.0 %copy.10 = s32[524288]{0:T(1024)} copy(s32[524288]{0:T(1024)} %bitcast.14) | data formatting | bytes 4194304
